TPU v7x, 256 devices: a whole 4x4x8 slice. The times are simulated.
256 devices in a mesh: seq: 64 (over z, y, core), head: 4 (over x).
Axes of the slice: x: 4, y: 4, z: 8, core: 2. Of those that a mesh axis runs over, the one named last changes fastest.
Arguments:
- layer_in: bfloat16 [32768, 2048], P('seq', 'head'), may hold values from -6 to 6
- query_weight: bfloat16 [2048, 1024], P(None, 'head'), may hold values from -0.125 to 0.125
- key_weight: bfloat16 [2048, 1024], P(None, 'head'), may hold values from -0.125 to 0.125
- value_weight: bfloat16 [2048, 1024], P(None, 'head'), may hold values from -0.125 to 0.125
- gate_weight: bfloat16 [2048, 1024], P(None, 'head'), may hold values from -0.125 to 0.125
- beta_weight: bfloat16 [2048, 8], P(None, 'head'), may hold values from -0.125 to 0.125
- decay_weight: bfloat16 [2048, 8], P(None, 'head'), may hold values from -0.125 to 0.125
- conv_weight: float32 [4, 3, 1024], P(None, None, 'head'), may hold values from -3 to 3
- decay_log: float32 [8], P('head'), as said below
- beta_bias: float32 [8], P('head'), as said below
- decay_bias: float32 [8], P('head'), may hold values from -1 to 1
- norm_gain: float32 [128], replicated, may hold values from 0.1 to 1.9
- out_weight: bfloat16 [1024, 2048], P('head'), may hold values from -0.1875 to 0.1875
Outputs:
- layer_out: bfloat16 [32768, 2048], P('seq', 'head')
Inputs may be any that keep to these rules, and one draw needn't show every extreme that they name: decay_log lies between log(0.1 / 32768) and log(0.05). beta_bias lies between log(0.5 * 128 / 32768) and 1.
All inputs are finite; a program needn't handle non-finite values.
Results may differ from a plain program's by a relative error of at most 0.0049.
Values may be sent and summed in bfloat16 or wider, within the bound.
A program may use at most 128 MiB of HBM per device.

v0:
```python
import jax
import jax.numpy as jnp
from jax import lax
from jax.sharding import Mesh
from jax.sharding import PartitionSpec as P

BLOCK = 128
SEQ = ("seq_0", "seq_1", "seq_2")
exact_mode = lax.Precision.HIGHEST
norm_floor = 0.0001


def passed_along(value, axis, steps):
    count = lax.axis_size(axis)
    leading, last = (max(0, -steps), min(count, count - steps))
    return lax.ppermute(value, axis, [(source, source + steps) for source in range(leading, last)])


def neutral_like(value, identity):
    return jax.tree.map(
        lambda part, zero: jnp.zeros_like(part) + jnp.asarray(zero, part.dtype), value, identity
    )


def carried_in(value, axes, combine, identity):
    before = start = neutral_like(value, identity)
    subtotal = value
    for axis in reversed(axes):
        length, mine = (lax.axis_size(axis), lax.axis_index(axis))
        pieces = jax.tree.map(lambda part: lax.all_gather(part, axis), subtotal)
        inside, subtotal = (start, start)
        for k in range(length):
            passed = k < mine
            subtotal = combine(subtotal, jax.tree.map(lambda part: part[k], pieces))
            inside = jax.tree.map(lambda new, old: jnp.where(passed, new, old), subtotal, inside)
        before = combine(inside, before)
    return before


def copy_for_each(value, axis):
    length = lax.axis_size(axis)
    return lax.all_to_all(
        jnp.broadcast_to(value[None], (length, *value.shape)), axis, 0, 0, tiled=True
    )


def in_order(tiles, dim):
    tiles = jnp.moveaxis(tiles, 0, dim)
    dims = tiles.shape
    return tiles.reshape(*dims[:dim], dims[dim] * dims[dim + 1], *dims[dim + 2 :])


def collect(value, axis, dim):
    tiles = copy_for_each(value, axis)
    return in_order(tiles, dim)


def causal_conv(values, earlier, kernel):
    reach_back = kernel.shape[0] - 1
    tokens = values.shape[0]
    extended = jnp.concatenate([earlier, values], axis=0)
    summed = kernel[0] * values
    for offset in range(1, reach_back + 1):
        summed = (
            summed + kernel[offset] * extended[reach_back - offset : reach_back - offset + tokens]
        )
    return jax.nn.silu(summed)


def unit_rows(values):
    return values * lax.rsqrt(jnp.sum(values * values, axis=-1, keepdims=True) + 1.0)


def unit_lower_inverse(system):
    length = system.shape[-1]
    row_index = lax.broadcasted_iota(jnp.int32, (length, length), 0)
    col_index = lax.broadcasted_iota(jnp.int32, (length, length), 1)
    inverse = jnp.broadcast_to(jnp.eye(length, dtype=jnp.float32), system.shape)
    width = 1
    while width < length:
        same_pair = row_index // (2 * width) == col_index // (2 * width)
        lower_half = row_index // width > col_index // width
        linking = jnp.where(same_pair & lower_half, system, 0.0)
        middle = lax.optimization_barrier(
            jnp.einsum("...rs,...st->...rt", linking, inverse, precision=exact_mode)
        )
        update = lax.optimization_barrier(
            jnp.einsum("...rs,...st->...rt", inverse, middle, precision=exact_mode)
        )
        inverse = inverse - update
        width = width * 2
    return inverse


def block_terms(queries, key_rows, values, beta_gate, log_decay):
    length = log_decay.shape[-1]
    running = jnp.cumsum(log_decay, axis=-1)
    row_index = lax.broadcasted_iota(jnp.int32, (length, length), 0)
    col_index = lax.broadcasted_iota(jnp.int32, (length, length), 1)
    within = row_index >= col_index
    before = row_index > col_index
    spread = running[..., :, None] - running[..., None, :]
    decay_matrix = jnp.where(within, jnp.exp(jnp.minimum(spread, 0.0)), 0.0)
    key_gram = jnp.einsum("...rd,...sd->...rs", key_rows, key_rows, precision=exact_mode)
    lower_part = jnp.where(before, beta_gate[..., :, None] * decay_matrix * key_gram, 0.0)
    system = lower_part + jnp.eye(length, dtype=jnp.float32)
    growth = jnp.exp(running)
    right_side = jnp.concatenate(
        [beta_gate[..., None] * values, (beta_gate * growth)[..., None] * key_rows], axis=-1
    )
    solved = jnp.einsum(
        "...rs,...se->...re", unit_lower_inverse(system), right_side, precision=exact_mode
    )
    value_dim = values.shape[-1]
    fixed_rows = solved[..., :value_dim]
    erased = solved[..., value_dim:]
    query_key = jnp.einsum("...rd,...sd->...rs", queries, key_rows, precision=exact_mode)
    mixing = jnp.where(within, decay_matrix * query_key, 0.0)
    local_out = jnp.einsum("...rs,...se->...re", mixing, fixed_rows, precision=exact_mode)
    removed = lax.optimization_barrier(
        jnp.einsum("...rs,...sd->...rd", mixing, erased, precision=exact_mode)
    )
    reader = growth[..., None] * queries - removed
    tail_decay = jnp.exp(running[..., -1:] - running)
    weighted = tail_decay[..., None] * key_rows
    key_dim = key_rows.shape[-1]
    lost_part = lax.optimization_barrier(
        jnp.einsum("...bd,...be->...de", weighted, erased, precision=exact_mode)
    )
    transit = (
        jnp.exp(running[..., -1])[..., None, None] * jnp.eye(key_dim, dtype=jnp.float32) - lost_part
    )
    carried = jnp.einsum("...bd,...be->...de", weighted, fixed_rows, precision=exact_mode)
    return (local_out, reader, transit, carried)


def compose(earlier, later_map):
    joined = jnp.einsum("...de,...ef->...df", later_map[0], earlier[0], precision=exact_mode)
    moved = (
        jnp.einsum("...de,...ef->...df", later_map[0], earlier[1], precision=exact_mode)
        + later_map[1]
    )
    return (joined, moved)


def on_device(
    layer_in,
    query_weight,
    key_weight,
    value_weight,
    gate_weight,
    beta_weight,
    decay_weight,
    conv_weight,
    decay_log,
    beta_bias,
    decay_bias,
    norm_gain,
    out_weight,
):
    tokens = layer_in.shape[0]
    head_count = beta_weight.shape[1]
    head_dim = query_weight.shape[1] // head_count
    weights = (query_weight, key_weight, value_weight, gate_weight, beta_weight, decay_weight)
    shard_piece = lax.all_gather(layer_in, "head", axis=1, tiled=True)
    query_raw, key_raw, value_raw, gate_raw, beta_raw, decay_raw = tuple(
        (jnp.dot(shard_piece, weight, preferred_element_type=jnp.float32) for weight in weights)
    )
    reach_back = conv_weight.shape[0] - 1
    channels = query_raw.shape[1]
    last_rows = jnp.concatenate(
        [
            query_raw[tokens - reach_back :],
            key_raw[tokens - reach_back :],
            value_raw[tokens - reach_back :],
        ],
        axis=1,
    )
    prior_rows = passed_along(last_rows, SEQ, 1)
    mixed_query = causal_conv(query_raw, prior_rows[:, :channels], conv_weight[:, 0])
    mixed_key = causal_conv(key_raw, prior_rows[:, channels : 2 * channels], conv_weight[:, 1])
    mixed_value = causal_conv(value_raw, prior_rows[:, 2 * channels :], conv_weight[:, 2])
    queries = unit_rows(mixed_query.reshape(tokens, head_count, head_dim))
    key_rows = unit_rows(mixed_key.reshape(tokens, head_count, head_dim))
    values = mixed_value.reshape(tokens, head_count, head_dim)
    beta_gate = jax.nn.sigmoid(beta_raw + beta_bias)
    log_decay = -jnp.exp(decay_log) * jax.nn.softplus(decay_raw + decay_bias)
    blocks = tokens // BLOCK

    def arrange(array):
        return array.reshape(blocks, BLOCK, head_count, head_dim).transpose(0, 2, 1, 3)

    def arrange_gate(array):
        return array.reshape(blocks, BLOCK, head_count).transpose(0, 2, 1)

    local_out, reader, transit, carried = block_terms(
        arrange(queries),
        arrange(key_rows),
        arrange(values),
        arrange_gate(beta_gate),
        arrange_gate(log_decay),
    )
    identity = jnp.broadcast_to(
        jnp.eye(head_dim, dtype=jnp.float32), (head_count, head_dim, head_dim)
    )
    nothing = jnp.zeros((head_count, head_dim, head_dim), jnp.float32)

    def through(running_pair, block_maps):
        return (compose(running_pair, block_maps), None)

    slab_pair, unused_rest = lax.scan(through, (identity, nothing), (transit, carried))
    slab_transit, slab_state = slab_pair
    scanned = carried_in((slab_transit, slab_state), SEQ, compose, (identity, nothing))
    incoming = scanned[1]

    def advance(carry_state, block_maps):
        following = (
            jnp.einsum("hde,hef->hdf", block_maps[0], carry_state, precision=exact_mode)
            + block_maps[1]
        )
        return (following, carry_state)

    unused_last, starts = lax.scan(advance, incoming, (transit, carried))
    outputs = local_out + jnp.einsum("nhrd,nhde->nhre", reader, starts, precision=exact_mode)
    head_out = outputs.transpose(0, 2, 1, 3).reshape(tokens, head_count, head_dim)
    gate_rows = gate_raw.reshape(tokens, head_count, head_dim)
    scaled = head_out * lax.rsqrt(
        jnp.mean(head_out * head_out, axis=-1, keepdims=True) + norm_floor
    )
    hidden = (
        (scaled * norm_gain * jax.nn.silu(gate_rows))
        .reshape(tokens, head_count * head_dim)
        .astype(jnp.bfloat16)
    )
    column_weight = lax.all_to_all(out_weight, "head", split_axis=1, concat_axis=0, tiled=True)
    summed = jnp.dot(collect(hidden, "head", 1), column_weight, preferred_element_type=jnp.float32)
    return summed.astype(jnp.bfloat16)


def solution(mesh):
    finer = Mesh(
        mesh.devices.reshape(8, 4, 2, mesh.shape["head"]), ("seq_0", "seq_1", "seq_2", "head")
    )
    return jax.shard_map(
        on_device,
        mesh=finer,
        in_specs=(
            P(SEQ, "head"),
            P(None, "head"),
            P(None, "head"),
            P(None, "head"),
            P(None, "head"),
            P(None, "head"),
            P(None, "head"),
            P(None, None, "head"),
            P("head"),
            P("head"),
            P("head"),
            P(),
            P("head", None),
        ),
        out_specs=P(SEQ, "head"),
        check_vma=False,
    )
```

profile of v0, /device:TPU:8, one launch (start us, length us, event | category | flops | bytes accessed | tf_op | source)
XLA Modules:
  0.0 231.8 jit_solution(16035866141420245483)
XLA Ops:
  10.7 34.6 %all-gather.10.cloned.1.call-done = bf16[512,2048]{1,0:T(8,128)(2,1)} async-done(((bf16[512,512]{1,0:T(8,128)(2,1)}), bf16[512,2048]{1,0:T(8,128)(2,1)}) %all-gather.10.cloned.1.call-update) | async-done | bytes 2097168 | tf_op jit(solution)/shard_map/all_gather | solution.py:165
  45.4 2.4 %fusion.166 = f32[4,2,128]{2,1,0:T(2,128)S(1)} fusion(bf16[512,2048]{1,0:T(8,128)(2,1)} %all-gather.10.cloned.1.call-done, bf16[2048,2]{0,1:T(2,128)(2,1)} %param.23, f32[2]{0:T(128)} %param.27, f32[2]{0:T(128)} %exponential_negate_fusion), kind=kOutput, calls=%fused_computation.232 | convolution fusion | flops 4202496 | bytes 2109456 | tf_op jit(solution)/shard_map/dot_general | solution.py:167
  52.8 2.1 collective-permute-start
  55.7 2.1 collective-permute-done
  76.4 2.2 fusion.26
  81.4 2.4 %while.28 = (s32[]{:T(128)}, f32[2,128,128]{2,1,0:T(8,128)S(1)}, f32[2,128,128]{2,1,0:T(8,128)S(1)}, f32[4,2,128,128]{3,2,1,0:T(8,128)S(1)}, f32[4,2,128,128]{3,2,1,0:T(8,128)S(1)}) while((s32[]{:T(128)}, f32[2,128,128]{2,1,0:T(8,128)S(1)}, f32[2,128,128]{2,1,0:T(8,128)S(1)}, f32[4,2,128,128]{3,2,1,0:T(8,128)S(1)}, ...), condition=%wide.region_4.5_spmd.clone.clone, body=%wide.region_3.4_spmd.clone.sunk.clone | while | flops 100728832 | bytes 1443410 | solution.py:211
  85.2 2.2 all-gather
  88.3 13.5 %all-gather.1 = f32[8,128,128]{2,1,0:T(8,128)S(1)} all-gather(f32[2,128,128]{2,1,0:T(8,128)S(1)} %fusion.195), channel_id=3, replica_groups=mesh['seq_0'=8,'seq_1'=4,'seq_2'=2,'head'=4] {'seq_1'}, dimensions={0}, use_global_device_ids=true | all-gather | bytes 655360 | tf_op jit(solution)/shard_map/all_gather | solution.py:30
  105.6 2.3 copy.83
  107.8 2.3 copy.84
  110.1 4.2 %all-to-all-start.1 = ((bf16[256,4,512]{2,0,1:T(8,128)(2,1)}), bf16[256,4,512]{2,0,1:T(8,128)(2,1)}, u32[]{:S(2)}, u32[]{:S(2)}) async-start(bf16[256,4,512]{2,0,1:T(8,128)(2,1)} %copy.84), calls=%async_computation.1 | async-start | bytes 2097152 | tf_op jit(solution)/shard_map/all_to_all | solution.py:235
  114.4 2.2 all-gather.3
  117.8 13.5 %all-gather.4 = f32[8,128,128]{2,1,0:T(8,128)S(1)} all-gather(f32[2,128,128]{2,1,0:T(8,128)S(1)} %convolution_add_fusion.13), channel_id=6, replica_groups=mesh['seq_0'=8,'seq_1'=4,'seq_2'=2,'head'=4] {'seq_1'}, dimensions={0}, use_global_device_ids=true | all-gather | bytes 655360 | tf_op jit(solution)/shard_map/all_gather | solution.py:30
  134.2 2.2 mul.279
  136.3 2.4 %reduce_sum.27 = f32[512,2]{1,0:T(8,128)} reduce(f32[512,2,128]{2,1,0:T(2,128)} %mul.279, f32[]{:T(128)} %constant.233.clone.1), dimensions={2}, to_apply=%region_1.2 | reduce | flops 130048 | bytes 528388 | tf_op jit(solution)/shard_map/reduce_sum | solution.py:71
  139.8 2.2 reshape.130
  142.0 2.5 %fusion.18 = f32[4,2,128,128]{3,2,1,0:T(8,128)S(1)} fusion(f32[4,128,2,128]{3,2,1,0:T(2,128)} %reshape.130, f32[4,128,2,128]{3,2,1,0:T(2,128)S(1)} %copy-done.2, f32[4,128,2]{1,2,0:T(2,128)S(1)} %bitcast.192, f32[4,128,2]{1,2,0:T(2,128)S(1)} %bitcast.193, f32[4,2,128]{2,1,0:T(2,128)S(1)} %reduce_window_sum.11, pred[128,128]{1,0:T(8,128)(4,1)S(1)} %get-tuple-element.135), kind=kOutput, calls=%fused_computation.25 | convolution fusion | flops 202244096 | bytes 1601536 | tf_op jit(solution)/shard_map/...rd,...sd->...rs/dot_general | solution.py:117
  148.8 35.7 %all-gather.14.cloned.1.call-done = f32[16,128,128]{2,1,0:T(8,128)} async-done(((f32[2,128,128]{2,1,0:T(8,128)}), f32[16,128,128]{2,1,0:T(8,128)}) %all-gather.14.cloned.1.call-update) | async-done | bytes 1048592 | tf_op jit(solution)/shard_map/all_gather | solution.py:30
  191.2 7.5 %while.27 = (s32[]{:T(128)}, f32[2,128,128]{2,1,0:T(8,128)S(1)}, f32[4,2,128,128]{3,2,1,0:T(8,128)}, f32[4,2,128,128]{3,2,1,0:T(8,128)S(1)}, f32[4,2,128,128]{3,2,1,0:T(8,128)}) while((s32[]{:T(128)}, f32[2,128,128]{2,1,0:T(8,128)S(1)}, f32[4,2,128,128]{3,2,1,0:T(8,128)}, f32[4,2,128,128]{3,2,1,0:T(8,128)S(1)}, ...), condition=%wide.region_6.7_spmd.clone, body=%wide.region_5.6_spmd.sunk.clone | while | flops 50364416 | bytes 1049673 | solution.py:223
  198.7 3.8 %multiply_reduce_fusion = (f32[4,128,2]{1,2,0:T(2,128)S(1)}, f32[4,128,2,128]{1,3,2,0:T(8,128)}) fusion(f32[4,2,128,128]{2,3,1,0:T(8,128)} %fusion.85, f32[4,2,128,128]{3,2,1,0:T(8,128)} %get-tuple-element.62, f32[4,2,128,128]{3,2,1,0:T(8,128)} %fusion.82, f32[4,128,2,128]{3,2,1,0:T(2,128)} %reshape.130, f32[4,2,128]{2,1,0:T(2,128)S(1)} %get-tuple-element.120, ...), kind=kOutput, calls=%fused_computation.103 | convolution fusion | flops 202112000 | bytes 2633728 | tf_op jit(solution)/shard_map/nhrd,nhde->nhre/dot_general | solution.py:224
  202.7 2.0 copy.81
  205.4 2.1 fusion.55
  207.6 14.9 %all_to_all.21 = bf16[4,512,256]{2,1,0:T(8,128)(2,1)S(1)} all-to-all(bf16[4,512,256]{2,1,0:T(8,128)(2,1)S(1)} %broadcast_in_dim.110), channel_id=1, replica_groups=mesh['seq_0'=8,'seq_1'=4,'seq_2'=2,'head'=4] {'head'}, dimensions={0} | all-to-all | bytes 2097152 | tf_op jit(solution)/shard_map/all_to_all | solution.py:42
  222.5 2.7 %fusion.14 = bf16[512,512]{1,0:T(8,128)(2,1)} fusion(bf16[256,4,512]{2,0,1:T(8,128)(2,1)} %all-to-all-done.1, bf16[4,512,256]{2,1,0:T(8,128)(2,1)S(1)} %all_to_all.21), kind=kOutput, calls=%fused_computation.18 | convolution fusion | flops 537133056 | bytes 2621440 | tf_op jit(solution)/shard_map/dot_general | solution.py:236
  (240 shorter events, 63.0 us)
Async XLA Ops:
  6.5 42.8 %copy-start = (bf16[2048,256]{1,0:T(8,128)(2,1)S(1)}, bf16[2048,256]{1,0:T(8,128)(2,1)}, u32[]{:S(2)}) copy-start(bf16[2048,256]{1,0:T(8,128)(2,1)} %param.20) | copy-start | bytes 3145732
  6.5 38.8 %all-gather.10.cloned.1.call-start = ((), (), s32[]{:S(2)}) async-start(), calls=%async_computation.2 | async-start | bytes 2621440 | tf_op jit(solution)/shard_map/all_gather | solution.py:165
  7.3 141.5 %all-gather.12.cloned.1.call-start = ((), (), s32[]{:S(2)}) async-start(), calls=%async_computation.3 | async-start | bytes 1179648 | tf_op jit(solution)/shard_map/all_gather | solution.py:30
  52.8 5.0 %collective-permute-start = (f32[3,768]{1,0:T(4,128)S(1)}, f32[3,768]{1,0:T(4,128)S(1)}, u32[]{:S(2)}, u32[]{:S(2)}) collective-permute-start(f32[3,768]{1,0:T(4,128)S(1)} %pad_maximum_fusion.3), channel_id=1, source_target_pairs={{0,4},{4,8},{8,12},{12,16},{16,20},{20,24},{24,28},{28,32},{32,36}... | collective-permute-start | bytes 27656 | tf_op jit(solution)/shard_map/ppermute | solution.py:16
  61.1 18.9 %copy-start.1 = (f32[4,128,2,128]{3,2,1,0:T(2,128)}, f32[4,128,2,128]{3,2,1,0:T(2,128)S(1)}, u32[]{:S(2)}) copy-start(f32[4,128,2,128]{3,2,1,0:T(2,128)S(1)} %reshape.131) | copy-start | bytes 1572868
  88.3 13.5 %copy-start.17 = (f32[2,128,128]{2,1,0:T(8,128)}, f32[2,128,128]{2,1,0:T(8,128)S(1)}, u32[]{:S(2)}) copy-start(f32[2,128,128]{2,1,0:T(8,128)S(1)} %fusion.195) | copy-start | bytes 393220
  110.1 97.4 %all-to-all-start.1 = ((bf16[256,4,512]{2,0,1:T(8,128)(2,1)}), bf16[256,4,512]{2,0,1:T(8,128)(2,1)}, u32[]{:S(2)}, u32[]{:S(2)}) async-start(bf16[256,4,512]{2,0,1:T(8,128)(2,1)} %copy.84), calls=%async_computation.1 | async-start | bytes 2097152 | tf_op jit(solution)/shard_map/all_to_all | solution.py:235
  114.4 70.2 %all-gather.14.cloned.1.call-start = ((), (), s32[]{:S(2)}) async-start(), calls=%async_computation.4 | async-start | bytes 1179648 | tf_op jit(solution)/shard_map/all_gather | solution.py:30
  117.5 16.6 %copy-start.50 = (f32[128]{0:T(128)S(1)}, f32[128]{0:T(128)}, u32[]{:S(2)}) copy-start(f32[128]{0:T(128)} %param.28) | copy-start | bytes 1540
  117.8 14.3 %copy-start.11 = (f32[2,128,128]{2,1,0:T(8,128)}, f32[2,128,128]{2,1,0:T(8,128)S(1)}, u32[]{:S(2)}) copy-start(f32[2,128,128]{2,1,0:T(8,128)S(1)} %convolution_add_fusion.13) | copy-start | bytes 393220
  134.1 7.9 %copy-start.2 = (f32[4,128,2,128]{3,2,1,0:T(2,128)S(1)}, f32[4,128,2,128]{3,2,1,0:T(2,128)}, u32[]{:S(2)}) copy-start(f32[4,128,2,128]{3,2,1,0:T(2,128)} %copy-done.1) | copy-start | bytes 1572868
  139.8 6.2 %copy-start.16 = (f32[2,128,128]{2,1,0:T(8,128)S(1)}, f32[2,128,128]{2,1,0:T(8,128)}, u32[]{:S(2)}) copy-start(f32[2,128,128]{2,1,0:T(8,128)} %copy-done.15) | copy-start | bytes 393220
  139.8 6.2 %copy-start.18 = (f32[2,128,128]{2,1,0:T(8,128)S(1)}, f32[2,128,128]{2,1,0:T(8,128)}, u32[]{:S(2)}) copy-start(f32[2,128,128]{2,1,0:T(8,128)} %copy-done.17) | copy-start | bytes 393220
  142.0 4.3 %copy-start.20 = (f32[2,128,128]{2,1,0:T(8,128)S(1)}, f32[2,128,128]{2,1,0:T(8,128)}, u32[]{:S(2)}) copy-start(f32[2,128,128]{2,1,0:T(8,128)} %convolution_add_fusion.10) | copy-start | bytes 393220
  142.0 4.4 %copy-start.28 = (f32[2,128,128]{2,1,0:T(8,128)S(1)}, f32[2,128,128]{2,1,0:T(8,128)}, u32[]{:S(2)}) copy-start(f32[2,128,128]{2,1,0:T(8,128)} %copy-done.27) | copy-start | bytes 393220
  142.0 4.4 %copy-start.30 = (f32[2,128,128]{2,1,0:T(8,128)S(1)}, f32[2,128,128]{2,1,0:T(8,128)}, u32[]{:S(2)}) copy-start(f32[2,128,128]{2,1,0:T(8,128)} %copy-done.29) | copy-start | bytes 393220
  142.0 4.4 %copy-start.32 = (f32[2,128,128]{2,1,0:T(8,128)S(1)}, f32[2,128,128]{2,1,0:T(8,128)}, u32[]{:S(2)}) copy-start(f32[2,128,128]{2,1,0:T(8,128)} %copy-done.31) | copy-start | bytes 393220
  142.0 4.7 %copy-start.19 = (f32[2,128,128]{2,1,0:T(8,128)S(1)}, f32[2,128,128]{2,1,0:T(8,128)}, u32[]{:S(2)}) copy-start(f32[2,128,128]{2,1,0:T(8,128)} %fusion.198) | copy-start | bytes 393220
  142.0 4.7 %copy-start.22 = (f32[2,128,128]{2,1,0:T(8,128)S(1)}, f32[2,128,128]{2,1,0:T(8,128)}, u32[]{:S(2)}) copy-start(f32[2,128,128]{2,1,0:T(8,128)} %copy-done.21) | copy-start | bytes 393220
  142.0 4.7 %copy-start.24 = (f32[2,128,128]{2,1,0:T(8,128)S(1)}, f32[2,128,128]{2,1,0:T(8,128)}, u32[]{:S(2)}) copy-start(f32[2,128,128]{2,1,0:T(8,128)} %copy-done.23) | copy-start | bytes 393220
  142.0 4.7 %copy-start.26 = (f32[2,128,128]{2,1,0:T(8,128)S(1)}, f32[2,128,128]{2,1,0:T(8,128)}, u32[]{:S(2)}) copy-start(f32[2,128,128]{2,1,0:T(8,128)} %copy-done.25) | copy-start | bytes 393220
  148.8 39.5 %copy-start.7 = (f32[16,128,128]{2,1,0:T(8,128)S(1)}, f32[16,128,128]{2,1,0:T(8,128)}, u32[]{:S(2)}) copy-start(f32[16,128,128]{2,1,0:T(8,128)} %all-gather.12.cloned.1.call-done) | copy-start | bytes 3145732
  184.5 5.0 %copy-start.33 = (f32[16,128,128]{2,1,0:T(8,128)S(1)}, f32[16,128,128]{2,1,0:T(8,128)}, u32[]{:S(2)}) copy-start(f32[16,128,128]{2,1,0:T(8,128)} %all-gather.14.cloned.1.call-done) | copy-start | bytes 3145732
  198.7 6.7 %copy-start.6 = (bf16[512,2048]{1,0:T(8,128)(2,1)S(1)}, bf16[512,2048]{1,0:T(8,128)(2,1)}, u32[]{:S(2)}) copy-start(bf16[512,2048]{1,0:T(8,128)(2,1)} %all-gather.10.cloned.1.call-done) | copy-start | bytes 6291460
  (32 other events, 69.1 us)
Sparse Core Ops, SparseCore 0:
  9.1 36.1 all-gather.9
  105.7 40.1 all-gather.11
  147.7 36.7 all-gather.13
where the time goes:
time: 233 us; the launch traced here: 232 us
  waiting for transfers between devices  73.2 us (31%)
  matrix products  54.7 us (23%)
  blocking collectives  46.3 us (20%)
  local copies, waits for them, and re-layouts  24.2 us (10%)
  between operations  14.3 us (6%)
  other arithmetic  12.4 us (5%)
  starting transfers between devices  6.43 us (3%)
    all_gather x2, waiting for transfers between devices, carried_in(): pieces = jax.tree.map(lambda part: lax.all_gather(part, axis), subtotal)  35.7 us
    all_gather x1, waiting for transfers between devices, on_device(): shard_piece = lax.all_gather(layer_in, 'head', axis=1, tiled=True)  34.6 us
    all_gather x4, blocking collectives, carried_in(): pieces = jax.tree.map(lambda part: lax.all_gather(part, axis), subtotal)  31.4 us
    all_to_all x1, blocking collectives, copy_for_each(): lax.all_to_all(jnp.broadcast_to(value[None], (length, *value.shape)), axi...  14.9 us
    dot_general x21, matrix products, compose(): jnp.einsum('...de,...ef->...df', later_map[0], earlier[1], precision=exac...  10.1 us
    unnamed x105, local copies, waits for them, and re-layouts  9.2 us
    dot_general x6, matrix products, on_device(): jnp.dot(shard_piece, weight, preferred_element_type=jnp.float32)  7.33 us
    dot_general x7, matrix products, unit_lower_inverse(): jnp.einsum('...rs,...st->...rt', inverse, middle, precision=exact_mode)  5.3 us
  transfers between devices with their start and end apart: 5, of which 3 were waited for; matrix products, arithmetic and copies ran while one was open for 21% of the time, Pallas kernels for 0%

commit v1 on v0

--- a/solution.py
+++ b/solution.py
@@ -162,7 +162,9 @@
     head_count = beta_weight.shape[1]
     head_dim = query_weight.shape[1] // head_count
     weights = (query_weight, key_weight, value_weight, gate_weight, beta_weight, decay_weight)
-    shard_piece = lax.all_gather(layer_in, "head", axis=1, tiled=True)
+    shard_piece = jnp.concatenate(
+        lax.all_to_all(jnp.stack([layer_in] * lax.axis_size("head")), "head", 0, 0), axis=1
+    )
     query_raw, key_raw, value_raw, gate_raw, beta_raw, decay_raw = tuple(
         (jnp.dot(shard_piece, weight, preferred_element_type=jnp.float32) for weight in weights)
     )

time: 233 us -> 240 us (1.030); the launches traced: 232 us -> 235 us
  waiting for transfers between devices: 73.2 us -> 67 us
  local copies, waits for them, and re-layouts: 24.2 us -> 30.1 us
  starting transfers between devices: 6.43 us -> 11 us
  matrix products: 54.7 us -> 51.5 us
    all_gather x1 -> x0, waiting for transfers between devices: 34.6 us -> none  [on_device(): shard_piece = lax.all_gather(layer_in, 'head', axis=1, tiled=True)]
    all_to_all x0 -> x1, waiting for transfers between devices: none -> 23.1 us  [on_device(): lax.all_to_all(jnp.stack([layer_in] * lax.axis_size('head')), 'head', 0, 0)]
    reshape x0 -> x4, local copies, waits for them, and re-layouts: none -> 9.86 us  [the longest x3 7.8 us: on_device(): jnp.concatenate(lax.all_to_all(jnp.stack([layer_in] * lax.axis_size('head...]
    all_gather x2, waiting for transfers between devices: 35.7 us -> 43.9 us  [carried_in(): pieces = jax.tree.map(lambda part: lax.all_gather(part, axis), subtotal)]
    all_to_all x0 -> x1, starting transfers between devices: none -> 4.42 us  [on_device(): lax.all_to_all(jnp.stack([layer_in] * lax.axis_size('head')), 'head', 0, 0)]
    unnamed x105 -> x113, local copies, waits for them, and re-layouts: 9.2 us -> 5.47 us
    another operation x0 -> x1, local copies, waits for them, and re-layouts: none -> 2.6 us  [on_device(): jnp.stack([layer_in] * lax.axis_size('head'))]
  transfers between devices with their start and end apart: 5 -> 5, of which waited for: 3 -> 3; matrix products, arithmetic and copies ran while one was open for 21% -> 24% of each run, Pallas kernels for 0% -> 0%
where the time goes in v1:
time: 240 us; the launch traced here: 235 us
  waiting for transfers between devices  67 us (28%)
  matrix products  51.5 us (21%)
  blocking collectives  46.8 us (20%)
  local copies, waits for them, and re-layouts  30.1 us (13%)
  between operations  14.9 us (6%)
  other arithmetic  13.8 us (6%)
  starting transfers between devices  11 us (5%)
    all_gather x2, waiting for transfers between devices, carried_in(): pieces = jax.tree.map(lambda part: lax.all_gather(part, axis), subtotal)  43.9 us
    all_gather x4, blocking collectives, carried_in(): pieces = jax.tree.map(lambda part: lax.all_gather(part, axis), subtotal)  31.8 us
    all_to_all x1, waiting for transfers between devices, on_device(): lax.all_to_all(jnp.stack([layer_in] * lax.axis_size('head')), 'head', 0, 0)  23.1 us
    all_to_all x1, blocking collectives, copy_for_each(): lax.all_to_all(jnp.broadcast_to(value[None], (length, *value.shape)), axi...  14.9 us
    dot_general x21, matrix products, compose(): jnp.einsum('...de,...ef->...df', later_map[0], earlier[1], precision=exac...  10.9 us
    reshape x3, local copies, waits for them, and re-layouts, on_device(): jnp.concatenate(lax.all_to_all(jnp.stack([layer_in] * lax.axis_size('head...  7.8 us
    dot_general x6, matrix products, on_device(): jnp.dot(shard_piece, weight, preferred_element_type=jnp.float32)  7.31 us
    unnamed x113, local copies, waits for them, and re-layouts  5.47 us
  transfers between devices with their start and end apart: 5, of which 3 were waited for; matrix products, arithmetic and copies ran while one was open for 24% of the time, Pallas kernels for 0%

profile of v1, /device:TPU:8, one launch (start us, length us, event | category | flops | bytes accessed | tf_op | source)
XLA Modules:
  0.0 235.3 jit_solution(13354847335281367759)
XLA Ops:
  6.5 2.6 %stack.2 = bf16[4,512,512]{2,1,0:T(8,128)(2,1)} broadcast(bf16[512,512]{1,0:T(8,128)(2,1)} %param.17), dimensions={1,2} | broadcast | bytes 2621440 | tf_op jit(solution)/shard_map/stack | solution.py:166
  9.1 4.4 %all-to-all-start = ((bf16[4,512,512]{2,1,0:T(8,128)(2,1)}), bf16[4,512,512]{2,1,0:T(8,128)(2,1)S(1)}, u32[]{:S(2)}, u32[]{:S(2)}) async-start(bf16[4,512,512]{2,1,0:T(8,128)(2,1)} %stack.2), calls=%async_computation | async-start | bytes 4194304 | tf_op jit(solution)/shard_map/all_to_all | solution.py:166
  16.8 23.1 %all-to-all-done = bf16[4,512,512]{2,1,0:T(8,128)(2,1)S(1)} async-done(((bf16[4,512,512]{2,1,0:T(8,128)(2,1)}), bf16[4,512,512]{2,1,0:T(8,128)(2,1)S(1)}, u32[]{:S(2)}, u32[]{:S(2)}) %all-to-all-start) | async-done | bytes 2097184 | tf_op jit(solution)/shard_map/all_to_all | solution.py:166
  49.4 2.3 fusion.182
  69.7 2.1 fusion.26
  74.6 2.4 %while.28 = (s32[]{:T(128)}, f32[2,128,128]{2,1,0:T(8,128)S(1)}, f32[2,128,128]{2,1,0:T(8,128)S(1)}, f32[4,2,128,128]{3,2,1,0:T(8,128)S(1)}, f32[4,2,128,128]{3,2,1,0:T(8,128)S(1)}) while((s32[]{:T(128)}, f32[2,128,128]{2,1,0:T(8,128)S(1)}, f32[2,128,128]{2,1,0:T(8,128)S(1)}, f32[4,2,128,128]{3,2,1,0:T(8,128)S(1)}, ...), condition=%wide.region_4.5_spmd.clone.clone, body=%wide.region_3.4_spmd.clone.sunk.clone | while | flops 100728832 | bytes 1442891 | solution.py:213
  77.0 3.3 %all-gather = f32[4,128,128]{2,1,0:T(8,128)S(1)} all-gather(f32[2,128,128]{2,1,0:T(8,128)S(1)} %get-tuple-element.60), channel_id=2, replica_groups=mesh['seq_0'=8,'seq_1'=4,'seq_2'=2,'head'=4] {'seq_2'}, dimensions={0}, use_global_device_ids=true | all-gather | bytes 393216 | tf_op jit(solution)/shard_map/all_gather | solution.py:30
  80.3 2.0 all-gather.3
  83.1 13.7 %all-gather.4 = f32[8,128,128]{2,1,0:T(8,128)S(1)} all-gather(f32[2,128,128]{2,1,0:T(8,128)S(1)} %convolution_add_fusion.13), channel_id=6, replica_groups=mesh['seq_0'=8,'seq_1'=4,'seq_2'=2,'head'=4] {'seq_1'}, dimensions={0}, use_global_device_ids=true | all-gather | bytes 655360 | tf_op jit(solution)/shard_map/all_gather | solution.py:30
  97.1 12.8 %all-gather.1 = f32[8,128,128]{2,1,0:T(8,128)S(1)} all-gather(f32[2,128,128]{2,1,0:T(8,128)S(1)} %fusion.192), channel_id=3, replica_groups=mesh['seq_0'=8,'seq_1'=4,'seq_2'=2,'head'=4] {'seq_1'}, dimensions={0}, use_global_device_ids=true | all-gather | bytes 655360 | tf_op jit(solution)/shard_map/all_gather | solution.py:30
  116.8 4.6 %all-to-all-start.2 = ((bf16[256,4,512]{2,0,1:T(8,128)(2,1)}), bf16[256,4,512]{2,0,1:T(8,128)(2,1)}, u32[]{:S(2)}, u32[]{:S(2)}) async-start(bf16[256,4,512]{2,0,1:T(8,128)(2,1)} %copy.66), calls=%async_computation.2 | async-start | bytes 2097152 | tf_op jit(solution)/shard_map/all_to_all | solution.py:237
  121.4 2.3 copy.69
  123.8 3.0 %copy.46 = bf16[512,4,512]{2,1,0:T(4,128)(2,1)} copy(bf16[512,4,512]{2,0,1:T(8,128)(2,1)S(1)} %bitcast.178) | data formatting | bytes 4194304 | tf_op jit(solution)/shard_map/reshape | solution.py:165
  126.7 4.5 %reshape.209 = bf16[512,2048,1]{1,0,2:T(8,128)(2,1)} reshape(bf16[512,4,512]{2,1,0:T(4,128)(2,1)} %copy.46) | data formatting | bytes 4194304 | tf_op jit(solution)/shard_map/reshape | solution.py:165
  132.3 2.5 %reduce_sum.27 = f32[512,2]{1,0:T(8,128)} reduce(f32[512,2,128]{2,1,0:T(2,128)} %mul.269, f32[]{:T(128)} %constant.233.clone.1), dimensions={2}, to_apply=%region_1.2 | reduce | flops 130048 | bytes 528388 | tf_op jit(solution)/shard_map/reduce_sum | solution.py:71
  138.7 2.5 %fusion.18 = f32[4,2,128,128]{3,2,1,0:T(8,128)S(1)} fusion(f32[4,128,2,128]{3,2,1,0:T(2,128)} %reshape.143, f32[4,128,2,128]{3,2,1,0:T(2,128)S(1)} %copy-done.8, f32[4,128,2]{1,2,0:T(2,128)S(1)} %bitcast.193, f32[4,128,2]{1,2,0:T(2,128)S(1)} %bitcast.194, f32[4,2,128]{2,1,0:T(2,128)S(1)} %reduce_window_sum.11, pred[128,128]{1,0:T(8,128)(4,1)S(1)} %get-tuple-element.135), kind=kOutput, calls=%fused_computation.25 | convolution fusion | flops 202244096 | bytes 1601536 | tf_op jit(solution)/shard_map/...rd,...sd->...rs/dot_general | solution.py:117
  144.8 5.3 %all-gather.11.cloned.1.call-done = f32[16,128,128]{2,1,0:T(8,128)} async-done(((f32[2,128,128]{2,1,0:T(8,128)}), f32[16,128,128]{2,1,0:T(8,128)}) %all-gather.11.cloned.1.call-update) | async-done | bytes 1048592 | tf_op jit(solution)/shard_map/all_gather | solution.py:30
  150.0 38.6 %all-gather.9.cloned.1.call-done = f32[16,128,128]{2,1,0:T(8,128)} async-done(((f32[2,128,128]{2,1,0:T(8,128)}), f32[16,128,128]{2,1,0:T(8,128)}) %all-gather.9.cloned.1.call-update) | async-done | bytes 1048592 | tf_op jit(solution)/shard_map/all_gather | solution.py:30
  195.4 7.7 %while.27 = (s32[]{:T(128)}, f32[2,128,128]{2,1,0:T(8,128)S(1)}, f32[4,2,128,128]{3,2,1,0:T(8,128)}, f32[4,2,128,128]{3,2,1,0:T(8,128)}, f32[4,2,128,128]{3,2,1,0:T(8,128)}) while((s32[]{:T(128)}, f32[2,128,128]{2,1,0:T(8,128)S(1)}, f32[4,2,128,128]{3,2,1,0:T(8,128)}, f32[4,2,128,128]{3,2,1,0:T(8,128)}, ...), condition=%wide.region_6.7_spmd.clone, body=%wide.region_5.6_spmd.sunk.clone | while | flops 50364416 | bytes 1050173 | solution.py:225
  203.2 2.0 multiply_reduce_fusion
  206.1 2.1 copy.62
  208.2 2.2 multiply_convert_fusion
  210.6 14.9 %all_to_all.26 = bf16[4,512,256]{2,1,0:T(8,128)(2,1)S(1)} all-to-all(bf16[4,512,256]{2,1,0:T(8,128)(2,1)S(1)} %broadcast_in_dim.110), channel_id=1, replica_groups=mesh['seq_0'=8,'seq_1'=4,'seq_2'=2,'head'=4] {'head'}, dimensions={0} | all-to-all | bytes 2097152 | tf_op jit(solution)/shard_map/all_to_all | solution.py:42
  225.5 2.7 %fusion.14 = bf16[512,512]{1,0:T(8,128)(2,1)} fusion(bf16[256,4,512]{2,0,1:T(8,128)(2,1)} %all-to-all-done.2, bf16[4,512,256]{2,1,0:T(8,128)(2,1)S(1)} %all_to_all.26), kind=kOutput, calls=%fused_computation.18 | convolution fusion | flops 537133056 | bytes 2621440 | tf_op jit(solution)/shard_map/dot_general | solution.py:238
  (251 shorter events, 66.5 us)
Async XLA Ops:
  6.5 34.7 %copy-start = (bf16[2048,256]{1,0:T(8,128)(2,1)S(1)}, bf16[2048,256]{1,0:T(8,128)(2,1)}, u32[]{:S(2)}) copy-start(bf16[2048,256]{1,0:T(8,128)(2,1)} %param.18) | copy-start | bytes 3145732
  9.1 5.7 %copy-start.40 = (f32[4,3,256]{2,0,1:T(4,128)S(1)}, f32[4,3,256]{2,0,1:T(4,128)}, u32[]{:S(2)}) copy-start(f32[4,3,256]{2,0,1:T(4,128)} %param.24) | copy-start | bytes 36868
  9.1 30.8 %all-to-all-start = ((bf16[4,512,512]{2,1,0:T(8,128)(2,1)}), bf16[4,512,512]{2,1,0:T(8,128)(2,1)S(1)}, u32[]{:S(2)}, u32[]{:S(2)}) async-start(bf16[4,512,512]{2,1,0:T(8,128)(2,1)} %stack.2), calls=%async_computation | async-start | bytes 4194304 | tf_op jit(solution)/shard_map/all_to_all | solution.py:166
  13.6 136.5 %all-gather.11.cloned.1.call-start = ((), (), s32[]{:S(2)}) async-start(), calls=%async_computation.4 | async-start | bytes 1179648 | tf_op jit(solution)/shard_map/all_gather | solution.py:30
  41.2 5.6 %copy-start.3 = (bf16[4,64,8,512]{3,2,0,1:T(8,128)(2,1)}, bf16[4,64,8,512]{3,2,0,1:T(8,128)(2,1)S(1)}, u32[]{:S(2)}) copy-start(bf16[4,64,8,512]{3,2,0,1:T(8,128)(2,1)S(1)} %copy.70) | copy-start | bytes 6291460
  44.0 5.4 %copy-start.42 = (bf16[2048,2]{0,1:T(2,128)(2,1)S(1)}, bf16[2048,2]{0,1:T(2,128)(2,1)}, u32[]{:S(2)}) copy-start(bf16[2048,2]{0,1:T(2,128)(2,1)} %param.22) | copy-start | bytes 24580
  44.8 6.9 %copy-start.36 = (f32[512,256]{1,0:T(8,128)}, f32[512,256]{1,0:T(8,128)S(1)}, u32[]{:S(2)}) copy-start(f32[512,256]{1,0:T(8,128)S(1)} %fusion.185) | copy-start | bytes 1572868
  44.8 7.0 %copy-start.44 = (f32[1,1,256]{2,0,1:T(1,128)S(1)}, f32[1,1,256]{2,0,1:T(1,128)}, u32[]{:S(2)}) copy-start(f32[1,1,256]{2,0,1:T(1,128)} %get-tuple-element.107) | copy-start | bytes 3076
  44.8 7.0 %copy-start.45 = (f32[1,1,256]{2,0,1:T(1,128)S(1)}, f32[1,1,256]{2,0,1:T(1,128)}, u32[]{:S(2)}) copy-start(f32[1,1,256]{2,0,1:T(1,128)} %get-tuple-element.108) | copy-start | bytes 3076
  44.8 7.0 %copy-start.46 = (f32[1,1,256]{2,0,1:T(1,128)S(1)}, f32[1,1,256]{2,0,1:T(1,128)}, u32[]{:S(2)}) copy-start(f32[1,1,256]{2,0,1:T(1,128)} %get-tuple-element.109) | copy-start | bytes 3076
  44.8 7.0 %copy-start.47 = (f32[1,1,256]{2,0,1:T(1,128)S(1)}, f32[1,1,256]{2,0,1:T(1,128)}, u32[]{:S(2)}) copy-start(f32[1,1,256]{2,0,1:T(1,128)} %get-tuple-element.110) | copy-start | bytes 3076
  44.8 7.0 %collective-permute-start = (f32[3,768]{1,0:T(4,128)S(1)}, f32[3,768]{1,0:T(4,128)S(1)}, u32[]{:S(2)}, u32[]{:S(2)}) collective-permute-start(f32[3,768]{1,0:T(4,128)S(1)} %pad_maximum_fusion.3), channel_id=1, source_target_pairs={{0,4},{4,8},{8,12},{12,16},{16,20},{20,24},{24,28},{28,32},{32,36}... | collective-permute-start | bytes 27656 | tf_op jit(solution)/shard_map/ppermute | solution.py:16
  53.5 19.6 %copy-start.7 = (f32[4,128,2,128]{3,2,1,0:T(2,128)}, f32[4,128,2,128]{3,2,1,0:T(2,128)S(1)}, u32[]{:S(2)}) copy-start(f32[4,128,2,128]{3,2,1,0:T(2,128)S(1)} %reshape.144) | copy-start | bytes 1572868
  77.0 19.9 %copy-start.4 = (f32[4,2,128,128]{3,2,1,0:T(8,128)}, f32[4,2,128,128]{3,2,1,0:T(8,128)S(1)}, u32[]{:S(2)}) copy-start(f32[4,2,128,128]{3,2,1,0:T(8,128)S(1)} %get-tuple-element.276) | copy-start | bytes 1572868
  77.0 32.9 %copy-start.10 = (f32[4,2,128,128]{3,2,1,0:T(8,128)}, f32[4,2,128,128]{3,2,1,0:T(8,128)S(1)}, u32[]{:S(2)}) copy-start(f32[4,2,128,128]{3,2,1,0:T(8,128)S(1)} %get-tuple-element.280) | copy-start | bytes 1572868
  82.6 27.9 %copy-start.15 = (f32[2,128,128]{2,1,0:T(8,128)}, f32[2,128,128]{2,1,0:T(8,128)S(1)}, u32[]{:S(2)}) copy-start(f32[2,128,128]{2,1,0:T(8,128)S(1)} %fusion.140) | copy-start | bytes 393220
  97.1 15.6 %copy-start.17 = (f32[2,128,128]{2,1,0:T(8,128)}, f32[2,128,128]{2,1,0:T(8,128)S(1)}, u32[]{:S(2)}) copy-start(f32[2,128,128]{2,1,0:T(8,128)S(1)} %fusion.192) | copy-start | bytes 393220
  112.1 76.5 %all-gather.9.cloned.1.call-start = ((), (), s32[]{:S(2)}) async-start(), calls=%async_computation.3 | async-start | bytes 1179648 | tf_op jit(solution)/shard_map/all_gather | solution.py:30
  116.8 7.0 %copy-start.2 = (bf16[4,512,512]{2,1,0:T(8,128)(2,1)S(1)}, bf16[4,512,512]{2,1,0:T(8,128)(2,1)}, u32[]{:S(2)}) copy-start(bf16[4,512,512]{2,1,0:T(8,128)(2,1)} %copy-done.1) | copy-start | bytes 6291460
  116.8 93.7 %all-to-all-start.2 = ((bf16[256,4,512]{2,0,1:T(8,128)(2,1)}), bf16[256,4,512]{2,0,1:T(8,128)(2,1)}, u32[]{:S(2)}, u32[]{:S(2)}) async-start(bf16[256,4,512]{2,0,1:T(8,128)(2,1)} %copy.66), calls=%async_computation.2 | async-start | bytes 2097152 | tf_op jit(solution)/shard_map/all_to_all | solution.py:237
  131.3 6.3 %copy-start.11 = (f32[512,256]{1,0:T(8,128)S(1)}, f32[512,256]{1,0:T(8,128)}, u32[]{:S(2)}) copy-start(f32[512,256]{1,0:T(8,128)} %get-tuple-element.102) | copy-start | bytes 1572868
  131.3 7.4 %copy-start.8 = (f32[4,128,2,128]{3,2,1,0:T(2,128)S(1)}, f32[4,128,2,128]{3,2,1,0:T(2,128)}, u32[]{:S(2)}) copy-start(f32[4,128,2,128]{3,2,1,0:T(2,128)} %copy-done.7) | copy-start | bytes 1572868
  132.3 8.9 %copy-start.6 = (f32[4,2,128,256]{3,2,1,0:T(8,128)S(1)}, f32[4,2,128,256]{3,2,1,0:T(8,128)}, u32[]{:S(2)}) copy-start(f32[4,2,128,256]{3,2,1,0:T(8,128)} %copy-done.5) | copy-start | bytes 3145732
  195.4 7.8 %copy-start.13 = (f32[4,128,2,128]{3,2,1,0:T(2,128)S(1)}, f32[4,128,2,128]{3,2,1,0:T(2,128)}, u32[]{:S(2)}) copy-start(f32[4,128,2,128]{3,2,1,0:T(2,128)} %reshape.143) | copy-start | bytes 1572868
  (36 other events, 109.7 us)
Sparse Core Ops, SparseCore 0:
  112.2 37.7 all-gather.10
  151.8 36.7 all-gather.8
